TPU v7x, 32 devices: a whole 2x2x4 slice. The times are simulated.
32 devices in a mesh: ta: 4 (over y, x), sa: 8 (over z, core).
Axes of the slice: x: 2, y: 2, z: 4, core: 2. Of those that a mesh axis runs over, the one named last changes fastest.
Arguments:
- eigvecs: float32 [2, 8, 64, 3, 4096], P(None, 'ta', None, None, 'sa'), may hold values from -0.0546875 to 0.0546875
- solutions: float32 [2, 8, 3, 8, 4, 3, 4096], P(None, 'ta', None, None, None, None, 'sa'), may hold values from -15 to 15
- source_times: int32 [3], replicated, may hold values from 0 to 7, as said below
- spin_dilution: int32 [3, 8], replicated, may hold values from 0 to 3
Outputs:
- perambulator: float32 [2, 8, 6144], P(None, 'ta', 'sa')
- norms: float32 [3, 8], replicated
Inputs may be any that keep to these rules, and one draw needn't show every extreme that they name: `source_times`: some source lies at slice 0 and another at slice 8 - 1.
All inputs are finite; a program needn't handle non-finite values.
Results may differ from a plain program's by a relative error of at most 0.000084.
Values sent between devices are 32-bit elements; how exact they have to be, the bound alone decides.
No kernel may reach another device: no remote copies, remote signals or barrier semaphores. Data moves between devices by JAX's collectives and lax.ppermute only.
A program may use at most 64 MiB of HBM per device.

v0:
```python
import jax
import jax.numpy as jnp
from jax import lax
from jax.sharding import PartitionSpec as P


def on_device(eigvecs, solutions, source_times, spin_dilution):
    time_rows = eigvecs.shape[1]
    eig_count = eigvecs.shape[2]
    site_count = eigvecs.shape[4]
    src_count = spin_dilution.shape[0]
    col_count = spin_dilution.shape[1]
    columns = src_count * col_count * 4
    inner_len = 3 * site_count
    all_cells = 12.0 * time_rows * lax.axis_size("ta") * site_count * lax.axis_size("sa")
    norm_parts = jnp.sum(solutions * solutions, axis=(0, 1, 4, 5, 6))
    eigen_rows = eigvecs.reshape(2, time_rows, eig_count, inner_len)
    solution_rows = solutions.reshape(2, time_rows, columns, inner_len)
    precise = lax.Precision.HIGHEST
    upper_half = jnp.concatenate([eigen_rows[0], eigen_rows[1]], axis=2)
    lower_half = jnp.concatenate([-eigen_rows[1], eigen_rows[0]], axis=2)
    left_side = jnp.concatenate([upper_half, lower_half], axis=1)
    right_side = jnp.concatenate([solution_rows[0], solution_rows[1]], axis=2)
    stacked = jnp.einsum(
        "tmk,tnk->tmn", left_side, right_side, precision=precise, preferred_element_type=jnp.float32
    )
    real_part = stacked[:, :eig_count]
    imag_part = stacked[:, eig_count:]
    slice_times = lax.axis_index("ta") * time_rows + jnp.arange(time_rows, dtype=jnp.int32)
    boundary = jnp.where(slice_times[:, None] < source_times[None, :], -1.0, 1.0).astype(
        jnp.float32
    )
    chirality = jnp.where(spin_dilution < 2, 1.0, -1.0).astype(jnp.float32)
    signs = jnp.broadcast_to(
        (boundary[:, :, None] * chirality[None])[:, :, :, None],
        (time_rows, src_count, col_count, 4),
    ).reshape(time_rows, columns)
    partial_value = (jnp.stack([real_part, imag_part]) * signs[None, :, None, :]).reshape(
        2, time_rows, eig_count * columns
    )
    own_width = eig_count * columns // lax.axis_size("sa")
    own_start = lax.axis_index("sa") * own_width
    norm_total = lax.psum(norm_parts, ("ta", "sa"))
    summed = lax.psum(partial_value, "sa")
    perambulator = lax.dynamic_slice_in_dim(summed, own_start, own_width, 2)
    return (perambulator, norm_total / all_cells)


def solution(mesh):
    return jax.shard_map(
        on_device,
        mesh=mesh,
        in_specs=(
            P(None, "ta", None, None, "sa"),
            P(None, "ta", None, None, None, None, "sa"),
            P(),
            P(),
        ),
        out_specs=(P(None, "ta", "sa"), P()),
        check_vma=False,
    )
```

profile of v0, /device:TPU:8, one launch (start us, length us, event | category | flops | bytes accessed | tf_op | source)
XLA Modules:
  0.0 92.8 jit_solution(17779468733230858066)
XLA Ops:
  7.2 0.0 all-reduce.2.cloned.1.call-start
  7.2 0.0 copy-start
  7.2 3.3 %fusion.12 = (f32[1,2,3,8,4,3,512]{6,4,5,3,2,1,0:T(4,128)S(1)}, f32[1,2,3,8,4,3,512]{6,4,5,3,2,1,0:T(4,128)}) fusion(f32[2,2,3,8,4,3,512]{6,4,5,3,2,1,0:T(4,128)} %param.5), kind=kLoop, calls=%fused_computation.20 | loop fusion | bytes 4718592 | tf_op jit(solution)/shard_map/slice | solution.py:23
  10.6 0.0 copy-done
  10.6 0.0 copy-start.1
  10.6 0.6 multiply_reduce_fusion
  11.1 0.8 copy-done.1
  12.0 0.1 fusion.13
  12.1 0.5 copy.10
  12.6 1.5 %squeeze.14 = f32[2,64,1536]{2,1,0:T(8,128)} reshape(f32[1,2,64,3,512]{4,3,2,1,0:T(4,128)S(1)} %copy.10) | data formatting | bytes 1572864 | tf_op jit(solution)/shard_map/squeeze | solution.py:20
  14.1 0.5 copy.11
  14.7 0.6 squeeze.15
  15.3 0.9 %neg.3 = f32[2,64,1536]{2,1,0:T(8,128)} negate(f32[2,64,1536]{2,1,0:T(8,128)S(1)} %squeeze.15) | non-fusion elementwise | flops 196608 | bytes 1572864 | tf_op jit(solution)/shard_map/neg | solution.py:21
  16.2 1.9 %copy.13 = f32[1,2,3,8,4,3,512]{6,5,4,3,2,1,0:T(4,128)S(1)} copy(f32[1,2,3,8,4,3,512]{6,4,5,3,2,1,0:T(4,128)} %get-tuple-element.3) | data formatting | bytes 2359296 | tf_op jit(solution)/shard_map/slice | solution.py:23
  18.1 1.7 %squeeze.17 = f32[2,96,1536]{2,1,0:T(8,128)} reshape(f32[1,2,3,8,4,3,512]{6,5,4,3,2,1,0:T(4,128)S(1)} %copy.13) | data formatting | bytes 2359296 | tf_op jit(solution)/shard_map/squeeze | solution.py:23
  19.9 0.7 copy.12
  20.5 0.0 copy-start.2
  20.6 1.7 %squeeze.16 = f32[2,96,1536]{2,1,0:T(8,128)} reshape(f32[1,2,3,8,4,3,512]{6,5,4,3,2,1,0:T(4,128)S(1)} %copy.12) | data formatting | bytes 2359296 | tf_op jit(solution)/shard_map/squeeze | solution.py:23
  22.3 0.0 copy-done.2
  22.3 0.0 copy-start.3
  22.3 0.0 copy-start.4
  22.3 5.4 %fusion = f32[2,128,96]{1,2,0:T(8,128)S(1)} fusion(f32[2,64,1536]{2,1,0:T(8,128)} %squeeze.14, f32[2,64,1536]{2,1,0:T(8,128)} %neg.3, f32[2,64,1536]{2,1,0:T(8,128)S(1)} %squeeze.15, f32[2,96,1536]{2,1,0:T(8,128)S(1)} %copy-done.2, f32[2,96,1536]{2,1,0:T(8,128)} %squeeze.16), kind=kOutput, calls=%fused_computation | convolution fusion | flops 908918784 | bytes 4816896 | tf_op jit(solution)/shard_map/tmk,tnk->tmn/dot_general | solution.py:24
  27.6 0.1 fusion.14
  27.7 0.1 copy.15
  27.8 0.1 stack.10
  28.0 0.1 copy.14
  28.0 0.1 stack.9
  28.2 0.0 copy-done.3
  28.2 0.0 copy-done.4
  28.2 0.1 compare_select_fusion.1
  28.3 0.1 broadcast_multiply_fusion
  28.4 0.1 broadcast_in_dim.30
  28.4 0.1 mul.45
  28.6 0.1 mul.47
  28.7 0.7 maximum_multiply_fusion
  29.4 0.0 all-reduce.2.cloned.1.call-update
  29.4 40.5 %psum.15 = f32[3,8]{1,0:T(4,128)S(1)} all-reduce(f32[3,8]{1,0:T(4,128)S(1)} %multiply_reduce_fusion), channel_id=1, replica_groups=mesh['ta'=4,'sa'=8] {'ta','sa'}, use_global_device_ids=true, to_apply=%region_2.3 | all-reduce | flops 24 | bytes 192 | tf_op jit(solution)/shard_map/psum | solution.py:43
  69.9 0.6 broadcast_multiply_fusion.1
  70.4 14.2 %all-reduce.2.cloned.1.call-done = f32[2,2,6144]{2,1,0:T(2,128)} async-done(((f32[2,2,6144]{2,1,0:T(2,128)}), f32[2,2,6144]{2,1,0:T(2,128)}) %all-reduce.2.cloned.1.call-update) | async-done | bytes 98320 | tf_op jit(solution)/shard_map/psum | solution.py:44
  84.7 1.3 %constant_dynamic-slice_fusion = f32[2,2,768]{2,1,0:T(2,128)} fusion(f32[2,2,6144]{2,1,0:T(2,128)} %all-reduce.2.cloned.1.call-done, s32[]{:T(128)S(6)} %select_n.17), kind=kLoop, calls=%fused_computation.18 | loop fusion | bytes 24580 | tf_op jit(solution)/shard_map/dynamic_slice | solution.py:45
  (3 shorter events, 0.0 us)
Async XLA Ops:
  7.2 77.5 %all-reduce.2.cloned.1.call-start = ((), (), s32[]{:S(2)}) async-start(), calls=%async_computation | async-start | bytes 196608 | tf_op jit(solution)/shard_map/psum | solution.py:44
  7.2 3.3 %copy-start = (f32[2,2,3,8,4,3,512]{6,4,5,3,2,1,0:T(4,128)S(1)}, f32[2,2,3,8,4,3,512]{6,4,5,3,2,1,0:T(4,128)}, u32[]{:S(2)}) copy-start(f32[2,2,3,8,4,3,512]{6,4,5,3,2,1,0:T(4,128)} %param.5) | copy-start | bytes 7077892
  10.6 1.4 %copy-start.1 = (f32[2,2,64,3,512]{4,2,3,1,0:T(8,128)S(1)}, f32[2,2,64,3,512]{4,2,3,1,0:T(8,128)}, u32[]{:S(2)}) copy-start(f32[2,2,64,3,512]{4,2,3,1,0:T(8,128)} %param.4) | copy-start | bytes 4718596
  20.5 1.7 %copy-start.2 = (f32[2,96,1536]{2,1,0:T(8,128)S(1)}, f32[2,96,1536]{2,1,0:T(8,128)}, u32[]{:S(2)}) copy-start(f32[2,96,1536]{2,1,0:T(8,128)} %squeeze.17) | copy-start | bytes 3538948
  22.3 5.9 %copy-start.3 = (s32[3,8]{1,0:T(4,128)S(1)}, s32[3,8]{1,0:T(4,128)}, u32[]{:S(2)}) copy-start(s32[3,8]{1,0:T(4,128)} %param.7) | copy-start | bytes 292
  22.3 5.9 %copy-start.4 = (s32[3]{0:T(128)S(1)}, s32[3]{0:T(128)}, u32[]{:S(2)}) copy-start(s32[3]{0:T(128)} %param.6) | copy-start | bytes 40
Sparse Core Ops, SparseCore 0:
  29.5 55.1 all-reduce.1
where the time goes:
time: 93.2 us; the launch traced here: 92.8 us
  blocking collectives  40.5 us (43%)
  local copies, waits for them, and re-layouts  15.6 us (17%)
  waiting for transfers between devices  14.3 us (15%)
  between operations  14.2 us (15%)
  matrix products  5.36 us (6%)
  other arithmetic  2.95 us (3%)
    psum x1, blocking collectives, on_device(): norm_total = lax.psum(norm_parts, ('ta', 'sa'))  40.5 us
    psum x1, waiting for transfers between devices, on_device(): summed = lax.psum(partial_value, 'sa')  14.2 us
    slice x3, local copies, waits for them, and re-layouts, on_device(): right_side = jnp.concatenate([solution_rows[0], solution_rows[1]], axis=2)  5.92 us
    dot_general x1, matrix products, on_device(): jnp.einsum('tmk,tnk->tmn', left_side, right_side, precision=precise, pref...  5.36 us
    squeeze x2, local copies, waits for them, and re-layouts, on_device(): right_side = jnp.concatenate([solution_rows[0], solution_rows[1]], axis=2)  3.46 us
    squeeze x2, local copies, waits for them, and re-layouts, on_device(): upper_half = jnp.concatenate([eigen_rows[0], eigen_rows[1]], axis=2)  2.07 us
  transfers between devices with their start and end apart: 1, of which 1 were waited for; matrix products, arithmetic and copies ran while one was open for 1% of the time, Pallas kernels for 0%

commit v1 on v0

--- a/solution.py
+++ b/solution.py
@@ -41,7 +41,7 @@
     own_width = eig_count * columns // lax.axis_size("sa")
     own_start = lax.axis_index("sa") * own_width
     norm_total = lax.psum(norm_parts, ("ta", "sa"))
-    summed = lax.psum(partial_value, "sa")
+    summed = jnp.sum(lax.all_gather(partial_value, "sa"), axis=0)
     perambulator = lax.dynamic_slice_in_dim(summed, own_start, own_width, 2)
     return (perambulator, norm_total / all_cells)
 

time: 93.2 us -> 87 us (0.933); the launches traced: 92.8 us -> 85.3 us
  blocking collectives: 40.5 us -> 56.1 us
  waiting for transfers between devices: 14.3 us -> 0 us
  between operations: 14.2 us -> 0.75 us
  local copies, waits for them, and re-layouts: 15.6 us -> 19 us
    all_gather x0 -> x1, blocking collectives: none -> 15.8 us  [on_device(): summed = jnp.sum(lax.all_gather(partial_value, 'sa'), axis=0)]
    psum x1 -> x0, waiting for transfers between devices: 14.2 us -> none  [on_device(): summed = lax.psum(partial_value, 'sa')]
    slice x3, local copies, waits for them, and re-layouts: 1.2 us -> 4.73 us  [on_device(): upper_half = jnp.concatenate([eigen_rows[0], eigen_rows[1]], axis=2)]
    squeeze x2, local copies, waits for them, and re-layouts: 3.46 us -> 5.76 us  [on_device(): right_side = jnp.concatenate([solution_rows[0], solution_rows[1]], axis=2)]
    slice x3, local copies, waits for them, and re-layouts: 5.92 us -> 4.1 us  [on_device(): right_side = jnp.concatenate([solution_rows[0], solution_rows[1]], axis=2)]
    neg x1, other arithmetic: 0.93 us -> 2.09 us  [on_device(): lower_half = jnp.concatenate([-eigen_rows[1], eigen_rows[0]], axis=2)]
  transfers between devices with their start and end apart: 1 -> 0, of which waited for: 1 -> 0; matrix products, arithmetic and copies ran while one was open for 1% -> 0% of each run, Pallas kernels for 0% -> 0%
where the time goes in v1:
time: 87 us; the launch traced here: 85.3 us
  blocking collectives  56.1 us (64%)
  local copies, waits for them, and re-layouts  19 us (22%)
  matrix products  5.72 us (7%)
  other arithmetic  3.79 us (4%)
    psum x1, blocking collectives, on_device(): norm_total = lax.psum(norm_parts, ('ta', 'sa'))  40.3 us
    all_gather x1, blocking collectives, on_device(): summed = jnp.sum(lax.all_gather(partial_value, 'sa'), axis=0)  15.8 us
    squeeze x2, local copies, waits for them, and re-layouts, on_device(): right_side = jnp.concatenate([solution_rows[0], solution_rows[1]], axis=2)  5.76 us
    dot_general x1, matrix products, on_device(): jnp.einsum('tmk,tnk->tmn', left_side, right_side, precision=precise, pref...  5.72 us
    slice x3, local copies, waits for them, and re-layouts, on_device(): upper_half = jnp.concatenate([eigen_rows[0], eigen_rows[1]], axis=2)  4.73 us
    slice x3, local copies, waits for them, and re-layouts, on_device(): right_side = jnp.concatenate([solution_rows[0], solution_rows[1]], axis=2)  4.1 us
    squeeze x2, local copies, waits for them, and re-layouts, on_device(): upper_half = jnp.concatenate([eigen_rows[0], eigen_rows[1]], axis=2)  2.99 us
    neg x1, other arithmetic, on_device(): lower_half = jnp.concatenate([-eigen_rows[1], eigen_rows[0]], axis=2)  2.09 us

profile of v1, /device:TPU:8, one launch (start us, length us, event | category | flops | bytes accessed | tf_op | source)
XLA Modules:
  0.0 85.3 jit_solution(319339221131711183)
XLA Ops:
  0.6 2.4 %fusion.13 = (f32[1,2,64,3,512]{4,2,3,1,0:T(8,128)}, f32[1,2,64,3,512]{4,2,3,1,0:T(8,128)S(1)}) fusion(f32[2,2,64,3,512]{4,2,3,1,0:T(8,128)} %param.4), kind=kLoop, calls=%fused_computation.21 | loop fusion | bytes 3145728 | tf_op jit(solution)/shard_map/slice | solution.py:20
  3.0 0.5 copy.16
  3.5 1.5 %squeeze.14 = f32[2,64,1536]{2,1,0:T(8,128)} reshape(f32[1,2,64,3,512]{4,3,2,1,0:T(4,128)S(1)} %copy.16) | data formatting | bytes 1572864 | tf_op jit(solution)/shard_map/squeeze | solution.py:20
  5.0 0.0 copy-start
  5.0 1.8 %copy.17 = f32[1,2,64,3,512]{4,3,2,1,0:T(4,128)S(1)} copy(f32[1,2,64,3,512]{4,2,3,1,0:T(8,128)} %get-tuple-element.4) | data formatting | bytes 1572864 | tf_op jit(solution)/shard_map/slice | solution.py:20
  6.8 1.5 %squeeze.15 = f32[2,64,1536]{2,1,0:T(8,128)} reshape(f32[1,2,64,3,512]{4,3,2,1,0:T(4,128)S(1)} %copy.17) | data formatting | bytes 1572864 | tf_op jit(solution)/shard_map/squeeze | solution.py:20
  8.4 2.1 %neg.3 = f32[2,64,1536]{2,1,0:T(8,128)} negate(f32[2,64,1536]{2,1,0:T(8,128)} %squeeze.15) | non-fusion elementwise | flops 196608 | bytes 1572864 | tf_op jit(solution)/shard_map/neg | solution.py:21
  10.4 0.0 copy-done
  10.5 0.5 fusion.12
  10.9 1.8 %copy.19 = f32[1,2,3,8,4,3,512]{6,5,4,3,2,1,0:T(4,128)} copy(f32[1,2,3,8,4,3,512]{6,4,5,3,2,1,0:T(4,128)S(1)} %get-tuple-element.3) | data formatting | bytes 2359296 | tf_op jit(solution)/shard_map/slice | solution.py:23
  12.8 2.8 %squeeze.17 = f32[2,96,1536]{2,1,0:T(8,128)} reshape(f32[1,2,3,8,4,3,512]{6,5,4,3,2,1,0:T(4,128)} %copy.19) | data formatting | bytes 2359296 | tf_op jit(solution)/shard_map/squeeze | solution.py:23
  15.6 1.8 %copy.18 = f32[1,2,3,8,4,3,512]{6,5,4,3,2,1,0:T(4,128)} copy(f32[1,2,3,8,4,3,512]{6,4,5,3,2,1,0:T(4,128)S(1)} %get-tuple-element.2) | data formatting | bytes 2359296 | tf_op jit(solution)/shard_map/slice | solution.py:23
  17.4 0.0 copy-start.1
  17.4 2.9 %squeeze.16 = f32[2,96,1536]{2,1,0:T(8,128)} reshape(f32[1,2,3,8,4,3,512]{6,5,4,3,2,1,0:T(4,128)} %copy.18) | data formatting | bytes 2359296 | tf_op jit(solution)/shard_map/squeeze | solution.py:23
  20.3 0.0 copy-done.1
  20.3 0.0 copy-start.2
  20.3 0.0 copy-start.3
  20.3 5.7 %fusion = f32[2,128,96]{1,2,0:T(8,128)S(1)} fusion(f32[2,64,1536]{2,1,0:T(8,128)} %squeeze.14, f32[2,64,1536]{2,1,0:T(8,128)} %neg.3, f32[2,64,1536]{2,1,0:T(8,128)S(1)} %copy-done.1, f32[2,96,1536]{2,1,0:T(8,128)} %squeeze.17, f32[2,96,1536]{2,1,0:T(8,128)} %squeeze.16), kind=kOutput, calls=%fused_computation | convolution fusion | flops 908918784 | bytes 4816896 | tf_op jit(solution)/shard_map/tmk,tnk->tmn/dot_general | solution.py:24
  26.1 0.1 fusion.14
  26.1 0.1 copy.21
  26.2 0.1 stack.10
  26.4 0.1 copy.20
  26.5 0.1 stack.9
  26.6 0.0 copy-done.2
  26.6 0.0 copy-done.3
  26.6 0.1 compare_select_fusion.1
  26.7 0.1 broadcast_multiply_fusion
  26.8 0.1 broadcast_in_dim.30
  26.8 0.1 mul.51
  27.0 0.1 mul.53
  27.1 0.1 maximum_multiply_fusion
  27.2 15.8 %all_gather.3 = f32[8,2,2,6144]{3,2,1,0:T(2,128)S(1)} all-gather(f32[1,2,2,6144]{3,2,1,0:T(2,128)S(1)} %maximum_multiply_fusion), channel_id=1, replica_groups=mesh['ta'=4,'sa'=8] {'sa'}, dimensions={0}, use_global_device_ids=true | all-gather | bytes 884736 | tf_op jit(solution)/shard_map/all_gather | solution.py:44
  42.9 0.3 reduce_sum.18
  43.2 0.6 constant_dynamic-slice_fusion
  43.8 0.6 multiply_reduce_fusion
  44.4 40.3 %psum.7 = f32[3,8]{1,0:T(4,128)S(1)} all-reduce(f32[3,8]{1,0:T(4,128)S(1)} %multiply_reduce_fusion), channel_id=1, replica_groups=mesh['ta'=4,'sa'=8] {'ta','sa'}, use_global_device_ids=true, to_apply=%region_2.3 | all-reduce | flops 24 | bytes 192 | tf_op jit(solution)/shard_map/psum | solution.py:43
  84.7 0.6 broadcast_multiply_fusion.1
  (3 shorter events, 0.0 us)
Async XLA Ops:
  5.0 5.4 %copy-start = (f32[2,2,3,8,4,3,512]{6,4,5,3,2,1,0:T(4,128)S(1)}, f32[2,2,3,8,4,3,512]{6,4,5,3,2,1,0:T(4,128)}, u32[]{:S(2)}) copy-start(f32[2,2,3,8,4,3,512]{6,4,5,3,2,1,0:T(4,128)} %param.5) | copy-start | bytes 7077892
  17.4 2.9 %copy-start.1 = (f32[2,64,1536]{2,1,0:T(8,128)S(1)}, f32[2,64,1536]{2,1,0:T(8,128)}, u32[]{:S(2)}) copy-start(f32[2,64,1536]{2,1,0:T(8,128)} %squeeze.15) | copy-start | bytes 2359300
  20.3 6.2 %copy-start.2 = (s32[3,8]{1,0:T(4,128)S(1)}, s32[3,8]{1,0:T(4,128)}, u32[]{:S(2)}) copy-start(s32[3,8]{1,0:T(4,128)} %param.7) | copy-start | bytes 292
  20.3 6.3 %copy-start.3 = (s32[3]{0:T(128)S(1)}, s32[3]{0:T(128)}, u32[]{:S(2)}) copy-start(s32[3]{0:T(128)} %param.6) | copy-start | bytes 40
